TPU v7x, 512 devices: a whole 4x4x16 slice. The times are simulated.
512 devices in a mesh: tau: 8 (over z_lo), row: 8 (over y, core), col: 8 (over x, z_hi).
Axes of the slice: x: 4, y: 4, z: 16 (z_hi: 2, z_lo: 8; z = z_hi * 8 + z_lo), core: 2. Of those that a mesh axis runs over, the one named last changes fastest.
Arguments:
- occupied: bfloat16 [8, 1024, 8192], P('tau', 'row', 'col'), may hold values from -6 to 6
- virtual_green: bfloat16 [8, 8192, 2048], P('tau', 'row', 'col'), may hold values from -0.0625 to 0.0625
- occ_mask: int32 [8, 64], P('row', 'col'), may hold values 0 or 1
- virt_mask: int32 [64, 16], P('row', 'col'), may hold values 0 or 1
- chi_mask: int32 [8, 16], P('row', 'col'), may hold values 0 or 1
- cosine_weights: float32 [8, 8], replicated, may hold values from -3 to 3
Outputs:
- chi_freq: float32 [8, 1024, 2048], P(None, ('row', 'tau'), 'col')
All inputs are finite; a program needn't handle non-finite values. No bound on the sum of `occ_mask` or of `virt_mask` or of `chi_mask` on one device may be relied on, other than what follows from the above.
Results may differ from a plain program's by a relative error of at most 0.0029.
Values may be sent and summed in bfloat16 or wider, within the bound.
A program may use at most 64 MiB of HBM per device.

v0:
```python
import jax
import jax.numpy as jnp
from jax import lax
from jax.sharding import PartitionSpec as P


def copy_for_each(value, axis):
    count = lax.axis_size(axis)
    return lax.all_to_all(
        jnp.broadcast_to(value[None], (count, *value.shape)), axis, 0, 0, tiled=True
    )


def joined_along(blocks, dim):
    shape = list(blocks.shape[1:])
    shape[dim] *= blocks.shape[0]
    return jnp.moveaxis(blocks, 0, dim).reshape(shape)


def collect(value, axis, dim):
    blocks = copy_for_each(value, axis)
    return joined_along(blocks, dim)


def expand_mask(values, flags):
    block_rows = values.shape[0] // flags.shape[0]
    block_cols = values.shape[1] // flags.shape[1]
    shaped = values.reshape(flags.shape[0], block_rows, flags.shape[1], block_cols)
    masked = shaped * flags.astype(values.dtype)[:, None, :, None]
    return masked.reshape(values.shape)


def shards(occupied, virtual_green, occ_mask, virt_mask, chi_mask, cosine_weights):
    occ_tile = expand_mask(occupied[0], occ_mask)
    virt_tile = expand_mask(virtual_green[0], virt_mask)
    virt_column = lax.all_gather(virt_tile, "row", axis=0, tiled=True)
    accumulated = jnp.dot(
        collect(occ_tile, "col", 1), virt_column, preferred_element_type=jnp.float32
    )
    chi_local = expand_mask(accumulated, chi_mask).astype(jnp.bfloat16)
    regrouped = lax.all_to_all(chi_local[None], "tau", split_axis=1, concat_axis=0, tiled=True)
    return jnp.einsum(
        "kt,tij->kij",
        cosine_weights,
        regrouped.astype(jnp.float32),
        precision=lax.Precision.HIGHEST,
    )


def solution(mesh):
    placed = (
        P("tau", "row", "col"),
        P("tau", "row", "col"),
        P("row", "col"),
        P("row", "col"),
        P("row", "col"),
        P(),
    )
    return jax.shard_map(
        shards,
        mesh=mesh,
        in_specs=placed,
        out_specs=P(None, ("row", "tau"), "col"),
        check_vma=False,
    )
```

profile of v0, /device:TPU:8, one launch (start us, length us, event | category | flops | bytes accessed | tf_op | source)
XLA Modules:
  0.0 165.8 jit_solution(2362016631813210816)
XLA Ops:
  6.5 0.0 copy-start
  6.5 0.7 convert_element_type.24
  7.3 0.1 copy.16
  7.4 0.3 mul.44
  7.7 1.9 %bitcast_multiply_fusion = bf16[1024,256]{1,0:T(8,128)(2,1)} fusion(bf16[128,8,2,128]{3,2,1,0:T(2,128)(2,1)S(1)} %bitcast.31, bf16[1,1024,256]{2,1,0:T(8,128)(2,1)} %param.7), kind=kLoop, calls=%fused_computation.3 | loop fusion | flops 262144 | bytes 1572864 | tf_op jit(solution)/shard_map/mul | solution.py:29
  9.6 0.0 all-gather.2.cloned.1.call-update
  9.7 0.0 copy-done.2
  9.7 0.1 broadcast_bitcast_fusion
  9.8 1.6 broadcast_in_dim.5
  11.4 17.7 %all-to-all-start = ((bf16[8,128,1024]{2,1,0:T(8,128)(2,1)}), bf16[8,128,1024]{2,1,0:T(8,128)(2,1)S(1)}, u32[]{:S(2)}, u32[]{:S(2)}) async-start(bf16[8,128,1024]{2,1,0:T(8,128)(2,1)} %broadcast_in_dim.5), calls=%async_computation | async-start | bytes 4194304 | tf_op jit(solution)/shard_map/all_to_all | solution.py:9
  29.1 23.8 %all-gather.2.cloned.1.call-done = bf16[8192,256]{1,0:T(8,128)(2,1)} async-done(((bf16[1024,256]{1,0:T(8,128)(2,1)}), bf16[8192,256]{1,0:T(8,128)(2,1)}) %all-gather.2.cloned.1.call-update) | async-done | bytes 4194320 | tf_op jit(solution)/shard_map/all_gather | solution.py:36
  52.9 6.4 %copy.17 = bf16[256,8192]{1,0:T(8,128)(2,1)} copy(bf16[256,8192]{0,1:T(8,128)(2,1)} %bitcast.30) | data formatting | bytes 8388608 | tf_op jit(solution)/shard_map/dot_general | solution.py:37
  59.3 19.7 %all-to-all-done = bf16[8,128,1024]{2,1,0:T(8,128)(2,1)S(1)} async-done(((bf16[8,128,1024]{2,1,0:T(8,128)(2,1)}), bf16[8,128,1024]{2,1,0:T(8,128)(2,1)S(1)}, u32[]{:S(2)}, u32[]{:S(2)}) %all-to-all-start) | async-done | bytes 2097184 | tf_op jit(solution)/shard_map/all_to_all | solution.py:9
  79.0 2.5 %copy.15 = bf16[128,8,1024]{2,1,0:T(8,128)(2,1)} copy(bf16[128,8,1024]{2,0,1:T(8,128)(2,1)S(1)} %bitcast.29) | data formatting | bytes 4194304 | tf_op jit(solution)/shard_map/transpose | solution.py:17
  81.5 2.9 %reshape.38 = bf16[128,8192,1]{1,0,2:T(8,128)(2,1)S(1)} reshape(bf16[128,8,1024]{2,1,0:T(8,128)(2,1)} %copy.15) | data formatting | bytes 4194304 | tf_op jit(solution)/shard_map/reshape | solution.py:17
  84.3 3.4 %fusion = bf16[128,2,128]{0,2,1:T(8,128)(2,1)S(1)} fusion(bf16[128,8192,1]{1,0,2:T(8,128)(2,1)S(1)} %reshape.38, bf16[2,128,8192]{2,1,0:T(8,128)(2,1)} %bitcast.28, f32[2]{0:T(128)S(1)} %convert_bitcast_fusion), kind=kOutput, calls=%fused_computation.2 | convolution fusion | flops 536936448 | bytes 6357000 | tf_op jit(solution)/shard_map/dot_general | solution.py:37
  87.8 0.1 copy.18
  87.9 0.5 broadcast.9
  88.4 1.0 reduce
  89.5 68.5 %all_to_all.17 = bf16[8,2,2048]{2,1,0:T(2,128)(2,1)S(1)} all-to-all(bf16[8,2,2048]{2,1,0:T(2,128)(2,1)S(1)} %reshape.41), channel_id=1, replica_groups=mesh['tau'=8,'row'=8,'col'=8] {'tau'}, dimensions={0} | all-to-all | bytes 131072 | tf_op jit(solution)/shard_map/all_to_all | solution.py:41
  158.0 0.1 reshape.42
  158.1 0.0 copy-done
  158.1 0.2 convolution_bitcast_fusion
  158.3 0.7 copy.20
  (11 shorter events, 0.1 us)
Async XLA Ops:
  6.5 151.6 %copy-start = (f32[8,8]{1,0:T(8,128)S(1)}, f32[8,8]{1,0:T(8,128)}, u32[]{:S(2)}) copy-start(f32[8,8]{1,0:T(8,128)} %param.11) | copy-start | bytes 772
  6.5 3.1 %copy-start.2 = (s32[1,8]{1,0:T(1,128)S(1)}, s32[1,8]{1,0:T(1,128)}, u32[]{:S(2)}) copy-start(s32[1,8]{1,0:T(1,128)} %param.8) | copy-start | bytes 100
  6.5 3.2 %copy-start.1 = (bf16[1,128,1024]{2,1,0:T(8,128)(2,1)S(1)}, bf16[1,128,1024]{2,1,0:T(8,128)(2,1)}, u32[]{:S(2)}) copy-start(bf16[1,128,1024]{2,1,0:T(8,128)(2,1)} %param.6) | copy-start | bytes 786436
  6.5 46.4 %all-gather.2.cloned.1.call-start = ((), (), s32[]{:S(2)}) async-start(), calls=%async_computation.2 | async-start | bytes 4718592 | tf_op jit(solution)/shard_map/all_gather | solution.py:36
  11.4 17.7 %copy-start.3 = (s32[1,2]{1,0:T(1,128)S(1)}, s32[1,2]{1,0:T(1,128)}, u32[]{:S(2)}) copy-start(s32[1,2]{1,0:T(1,128)} %param.10) | copy-start | bytes 28
  11.4 67.6 %all-to-all-start = ((bf16[8,128,1024]{2,1,0:T(8,128)(2,1)}), bf16[8,128,1024]{2,1,0:T(8,128)(2,1)S(1)}, u32[]{:S(2)}, u32[]{:S(2)}) async-start(bf16[8,128,1024]{2,1,0:T(8,128)(2,1)} %broadcast_in_dim.5), calls=%async_computation | async-start | bytes 4194304 | tf_op jit(solution)/shard_map/all_to_all | solution.py:9
Sparse Core Ops, SparseCore 0:
  9.8 43.0 all-gather.1
where the time goes:
time: 166 us
  blocking collectives  68.5 us (41%)
  waiting for transfers between devices  43.5 us (26%)
  starting transfers between devices  17.7 us (11%)
  local copies, waits for them, and re-layouts  15.3 us (9%)
  between operations  13.5 us (8%)
  other arithmetic  3.7 us (2%)
  matrix products  3.64 us (2%)
    all_to_all x1, blocking collectives, shards(): lax.all_to_all(chi_local[None], 'tau', split_axis=1, concat_axis=0, tiled...  68.5 us
    all_gather x1, waiting for transfers between devices, shards(): virt_column = lax.all_gather(virt_tile, 'row', axis=0, tiled=True)  23.8 us
    all_to_all x1, waiting for transfers between devices, copy_for_each(): lax.all_to_all(jnp.broadcast_to(value[None], (count, *value.shape)), axis...  19.7 us
    all_to_all x1, starting transfers between devices, copy_for_each(): lax.all_to_all(jnp.broadcast_to(value[None], (count, *value.shape)), axis...  17.7 us
    dot_general x1, local copies, waits for them, and re-layouts, shards(): jnp.dot(collect(occ_tile, 'col', 1), virt_column, preferred_element_type=...  6.39 us
    dot_general x1, matrix products, shards(): jnp.dot(collect(occ_tile, 'col', 1), virt_column, preferred_element_type=...  3.45 us
  transfers between devices with their start and end apart: 2, of which 2 were waited for; matrix products, arithmetic and copies ran while one was open for 5% of the time, Pallas kernels for 0%

commit v1 on v0

--- a/solution.py
+++ b/solution.py
@@ -2,6 +2,19 @@
 import jax.numpy as jnp
 from jax import lax
 from jax.sharding import PartitionSpec as P
+
+
+def gather_around(array, axis, dim):
+    ways = lax.axis_size(axis)
+    up = [(d, (d + 1) % ways) for d in range(ways)]
+    down = [(d, (d - 1) % ways) for d in range(ways)]
+    earlier, later = ([array], [array])
+    for _ in range(ways // 2):
+        earlier.append(lax.ppermute(earlier[-1], axis, up))
+    for _ in range((ways - 1) // 2):
+        later.append(lax.ppermute(later[-1], axis, down))
+    line = jnp.concatenate([*earlier[::-1], *later[1:]], axis=dim)
+    return jnp.roll(line, (lax.axis_index(axis) - ways // 2) * array.shape[dim], axis=dim)
 
 
 def copy_for_each(value, axis):
@@ -33,7 +46,7 @@
 def shards(occupied, virtual_green, occ_mask, virt_mask, chi_mask, cosine_weights):
     occ_tile = expand_mask(occupied[0], occ_mask)
     virt_tile = expand_mask(virtual_green[0], virt_mask)
-    virt_column = lax.all_gather(virt_tile, "row", axis=0, tiled=True)
+    virt_column = gather_around(virt_tile, "row", 0)
     accumulated = jnp.dot(
         collect(occ_tile, "col", 1), virt_column, preferred_element_type=jnp.float32
     )

time: 166 us -> 152 us (0.916)
  waiting for transfers between devices: 43.5 us -> 28.8 us
  between operations: 13.5 us -> 0.2 us
  local copies, waits for them, and re-layouts: 15.3 us -> 28.3 us
  blocking collectives: 68.5 us -> 62.6 us
  starting transfers between devices: 17.7 us -> 22.8 us
    ppermute x0 -> x7, waiting for transfers between devices: none -> 28.8 us  [the longest x4 28.5 us: gather_around(): earlier.append(lax.ppermute(earlier[-1], axis, up))]
    all_gather x1 -> x0, waiting for transfers between devices: 23.8 us -> none  [shards(): virt_column = lax.all_gather(virt_tile, 'row', axis=0, tiled=True)]
    all_to_all x1, waiting for transfers between devices: 19.7 us -> 0.01 us  [copy_for_each(): lax.all_to_all(jnp.broadcast_to(value[None], (count, *value.shape)), axis...]
    unnamed x12 -> x27, local copies, waits for them, and re-layouts: 0.63 us -> 11.3 us
    all_to_all x1, blocking collectives: 68.5 us -> 62.6 us  [shards(): lax.all_to_all(chi_local[None], 'tau', split_axis=1, concat_axis=0, tiled...]
    ppermute x0 -> x7, starting transfers between devices: none -> 5.23 us  [the longest x3 5.21 us: gather_around(): later.append(lax.ppermute(later[-1], axis, down))]
    dot_general x1 -> x2, local copies, waits for them, and re-layouts: 6.39 us -> 8.67 us  [shards(): jnp.dot(collect(occ_tile, 'col', 1), virt_column, preferred_element_type=...]
  transfers between devices with their start and end apart: 2 -> 8, of which waited for: 2 -> 5; matrix products, arithmetic and copies ran while one was open for 5% -> 14% of each run, Pallas kernels for 0% -> 0%
where the time goes in v1:
time: 152 us; the launch traced here: 151 us
  blocking collectives  62.6 us (41%)
  waiting for transfers between devices  28.8 us (19%)
  local copies, waits for them, and re-layouts  28.3 us (19%)
  starting transfers between devices  22.8 us (15%)
  other arithmetic  4.49 us (3%)
  matrix products  3.63 us (2%)
    all_to_all x1, blocking collectives, shards(): lax.all_to_all(chi_local[None], 'tau', split_axis=1, concat_axis=0, tiled...  62.6 us
    ppermute x4, waiting for transfers between devices, gather_around(): earlier.append(lax.ppermute(earlier[-1], axis, up))  28.5 us
    all_to_all x1, starting transfers between devices, copy_for_each(): lax.all_to_all(jnp.broadcast_to(value[None], (count, *value.shape)), axis...  17.6 us
    unnamed x27, local copies, waits for them, and re-layouts  11.3 us
    dot_general x2, local copies, waits for them, and re-layouts, shards(): jnp.dot(collect(occ_tile, 'col', 1), virt_column, preferred_element_type=...  8.67 us
    ppermute x3, starting transfers between devices, gather_around(): later.append(lax.ppermute(later[-1], axis, down))  5.21 us
    dot_general x1, matrix products, shards(): jnp.dot(collect(occ_tile, 'col', 1), virt_column, preferred_element_type=...  3.44 us
  transfers between devices with their start and end apart: 8, of which 5 were waited for; matrix products, arithmetic and copies ran while one was open for 14% of the time, Pallas kernels for 0%

profile of v1, /device:TPU:8, one launch (start us, length us, event | category | flops | bytes accessed | tf_op | source)
XLA Modules:
  0.0 150.8 jit_solution(9291422406510855570)
XLA Ops:
  1.7 1.6 %broadcast_in_dim.5 = bf16[8,128,1024]{2,1,0:T(8,128)(2,1)} broadcast(bf16[128,1024]{1,0:T(8,128)(2,1)S(1)} %multiply_bitcast_fusion), dimensions={1,2} | broadcast | bytes 2359296 | tf_op jit(solution)/shard_map/broadcast_in_dim | solution.py:23
  3.4 17.6 %all-to-all-start = ((bf16[8,128,1024]{2,1,0:T(8,128)(2,1)}), bf16[8,128,1024]{2,1,0:T(8,128)(2,1)S(1)}, u32[]{:S(2)}, u32[]{:S(2)}) async-start(bf16[8,128,1024]{2,1,0:T(8,128)(2,1)} %broadcast_in_dim.5), calls=%async_computation | async-start | bytes 4194304 | tf_op jit(solution)/shard_map/all_to_all | solution.py:22
  22.0 1.1 bitcast_multiply_fusion
  23.2 8.6 %collective-permute-done = bf16[1024,256]{1,0:T(8,128)(2,1)S(1)} collective-permute-done((bf16[1024,256]{1,0:T(8,128)(2,1)S(1)}, bf16[1024,256]{1,0:T(8,128)(2,1)S(1)}, u32[]{:S(2)}, u32[]{:S(2)}) %collective-permute-start) | collective-permute-done | bytes 524320 | tf_op jit(solution)/shard_map/ppermute | solution.py:13
  31.8 1.7 %collective-permute-start.4 = (bf16[1024,256]{1,0:T(8,128)(2,1)S(1)}, bf16[1024,256]{1,0:T(8,128)(2,1)}, u32[]{:S(2)}, u32[]{:S(2)}) collective-permute-start(bf16[1024,256]{1,0:T(8,128)(2,1)S(1)} %bitcast_multiply_fusion), channel_id=1, source_target_pairs={{0,56},{8,0},{16,8},{24,16},{32,24},{40,32},{48,40},{56,48},{1,57}... | collective-permute-start | bytes 1572872 | tf_op jit(solution)/shard_map/ppermute | solution.py:15
  33.5 6.9 %collective-permute-done.1 = bf16[1024,256]{1,0:T(8,128)(2,1)S(1)} collective-permute-done((bf16[1024,256]{1,0:T(8,128)(2,1)S(1)}, bf16[1024,256]{1,0:T(8,128)(2,1)S(1)}, u32[]{:S(2)}, u32[]{:S(2)}) %collective-permute-start.1) | collective-permute-done | bytes 524320 | tf_op jit(solution)/shard_map/ppermute | solution.py:13
  41.2 1.3 collective-permute-start.5
  42.5 6.7 %collective-permute-done.2 = bf16[1024,256]{1,0:T(8,128)(2,1)} collective-permute-done((bf16[1024,256]{1,0:T(8,128)(2,1)S(1)}, bf16[1024,256]{1,0:T(8,128)(2,1)}, u32[]{:S(2)}, u32[]{:S(2)}) %collective-permute-start.2) | collective-permute-done | bytes 524320 | tf_op jit(solution)/shard_map/ppermute | solution.py:13
  49.5 2.2 %collective-permute-start.6 = (bf16[1024,256]{1,0:T(8,128)(2,1)}, bf16[1024,256]{1,0:T(8,128)(2,1)S(1)}, u32[]{:S(2)}, u32[]{:S(2)}) collective-permute-start(bf16[1024,256]{1,0:T(8,128)(2,1)} %collective-permute-done.5), channel_id=1, source_target_pairs={{0,56},{8,0},{16,8},{24,16},{32,24},{40,32},{48,40},{56,48},{1,57}... | collective-permute-start | bytes 1572872 | tf_op jit(solution)/shard_map/ppermute | solution.py:15
  51.7 6.4 %collective-permute-done.3 = bf16[1024,256]{1,0:T(8,128)(2,1)} collective-permute-done((bf16[1024,256]{1,0:T(8,128)(2,1)}, bf16[1024,256]{1,0:T(8,128)(2,1)}, u32[]{:S(2)}, u32[]{:S(2)}) %collective-permute-start.3) | collective-permute-done | bytes 524320 | tf_op jit(solution)/shard_map/ppermute | solution.py:13
  59.1 1.1 constant_dynamic-update-slice_fusion.14
  60.2 1.1 constant_dynamic-update-slice_fusion.13
  61.4 1.1 constant_dynamic-update-slice_fusion.10
  62.5 1.1 constant_dynamic-update-slice_fusion.9
  63.6 1.1 constant_dynamic-update-slice_fusion.7
  64.7 1.1 constant_dynamic-update-slice_fusion.6
  65.9 1.1 constant_dynamic-update-slice_fusion.2
  67.0 1.1 constant_dynamic-update-slice_fusion.1
  68.1 2.2 %dynamic-slice_bitcast_fusion = bf16[256,8192]{0,1:T(8,128)(2,1)} fusion(bf16[16384,256]{1,0:T(8,128)(2,1)S(1)} %constant_dynamic-update-slice_fusion, s32[]{:T(128)S(6)} %select_n.14), kind=kLoop, calls=%fused_computation | loop fusion | bytes 8388612 | tf_op jit(solution)/shard_map/dot_general | solution.py:50
  70.3 6.4 %copy.17 = bf16[256,8192]{1,0:T(8,128)(2,1)} copy(bf16[256,8192]{0,1:T(8,128)(2,1)} %dynamic-slice_bitcast_fusion) | data formatting | bytes 8388608 | tf_op jit(solution)/shard_map/dot_general | solution.py:50
  76.8 2.5 %copy.15 = bf16[128,8,1024]{2,1,0:T(8,128)(2,1)} copy(bf16[128,8,1024]{2,0,1:T(8,128)(2,1)S(1)} %bitcast.30) | data formatting | bytes 4194304 | tf_op jit(solution)/shard_map/transpose | solution.py:30
  79.3 2.9 %reshape.38 = bf16[128,8192,1]{1,0,2:T(8,128)(2,1)S(1)} reshape(bf16[128,8,1024]{2,1,0:T(8,128)(2,1)} %copy.15) | data formatting | bytes 4194304 | tf_op jit(solution)/shard_map/reshape | solution.py:30
  82.1 3.4 %fusion = bf16[128,2,128]{0,2,1:T(8,128)(2,1)S(1)} fusion(bf16[128,8192,1]{1,0,2:T(8,128)(2,1)S(1)} %reshape.38, bf16[2,128,8192]{2,1,0:T(8,128)(2,1)} %bitcast.29, f32[2]{0:T(128)S(1)} %convert_bitcast_fusion), kind=kOutput, calls=%fused_computation.3 | convolution fusion | flops 536936448 | bytes 6357000 | tf_op jit(solution)/shard_map/dot_general | solution.py:50
  87.3 62.6 %all_to_all.17 = bf16[8,2,2048]{2,1,0:T(2,128)(2,1)S(1)} all-to-all(bf16[8,2,2048]{2,1,0:T(2,128)(2,1)S(1)} %reshape.41), channel_id=1, replica_groups=mesh['tau'=8,'row'=8,'col'=8] {'tau'}, dimensions={0} | all-to-all | bytes 131072 | tf_op jit(solution)/shard_map/all_to_all | solution.py:54
  (39 shorter events, 8.0 us)
Async XLA Ops:
  0.0 149.9 %copy-start = (f32[8,8]{1,0:T(8,128)S(1)}, f32[8,8]{1,0:T(8,128)}, u32[]{:S(2)}) copy-start(f32[8,8]{1,0:T(8,128)} %param.11) | copy-start | bytes 772
  0.0 49.1 %copy-start.3 = (s32[1,2]{1,0:T(1,128)S(1)}, s32[1,2]{1,0:T(1,128)}, u32[]{:S(2)}) copy-start(s32[1,2]{1,0:T(1,128)} %param.10) | copy-start | bytes 28
  3.4 73.4 %all-to-all-start = ((bf16[8,128,1024]{2,1,0:T(8,128)(2,1)}), bf16[8,128,1024]{2,1,0:T(8,128)(2,1)S(1)}, u32[]{:S(2)}, u32[]{:S(2)}) async-start(bf16[8,128,1024]{2,1,0:T(8,128)(2,1)} %broadcast_in_dim.5), calls=%async_computation | async-start | bytes 4194304 | tf_op jit(solution)/shard_map/all_to_all | solution.py:22
  23.2 8.6 %collective-permute-start = (bf16[1024,256]{1,0:T(8,128)(2,1)S(1)}, bf16[1024,256]{1,0:T(8,128)(2,1)S(1)}, u32[]{:S(2)}, u32[]{:S(2)}) collective-permute-start(bf16[1024,256]{1,0:T(8,128)(2,1)S(1)} %bitcast_multiply_fusion), channel_id=1, source_target_pairs={{0,8},{8,16},{16,24},{24,32},{32,40},{40,48},{48,56},{56,0},{1,9},... | collective-permute-start | bytes 1572872 | tf_op jit(solution)/shard_map/ppermute | solution.py:13
  31.8 8.6 %collective-permute-start.1 = (bf16[1024,256]{1,0:T(8,128)(2,1)S(1)}, bf16[1024,256]{1,0:T(8,128)(2,1)S(1)}, u32[]{:S(2)}, u32[]{:S(2)}) collective-permute-start(bf16[1024,256]{1,0:T(8,128)(2,1)S(1)} %collective-permute-done), channel_id=1, source_target_pairs={{0,8},{8,16},{16,24},{24,32},{32,40},{40,48},{48,56},{56,0},{1,9},... | collective-permute-start | bytes 1572872 | tf_op jit(solution)/shard_map/ppermute | solution.py:13
  31.8 8.6 %collective-permute-start.4 = (bf16[1024,256]{1,0:T(8,128)(2,1)S(1)}, bf16[1024,256]{1,0:T(8,128)(2,1)}, u32[]{:S(2)}, u32[]{:S(2)}) collective-permute-start(bf16[1024,256]{1,0:T(8,128)(2,1)S(1)} %bitcast_multiply_fusion), channel_id=1, source_target_pairs={{0,56},{8,0},{16,8},{24,16},{32,24},{40,32},{48,40},{56,48},{1,57}... | collective-permute-start | bytes 1572872 | tf_op jit(solution)/shard_map/ppermute | solution.py:15
  40.4 0.8 copy-start.1
  40.4 8.7 %collective-permute-start.2 = (bf16[1024,256]{1,0:T(8,128)(2,1)S(1)}, bf16[1024,256]{1,0:T(8,128)(2,1)}, u32[]{:S(2)}, u32[]{:S(2)}) collective-permute-start(bf16[1024,256]{1,0:T(8,128)(2,1)S(1)} %collective-permute-done.1), channel_id=1, source_target_pairs={{0,8},{8,16},{16,24},{24,32},{32,40},{40,48},{48,56},{56,0},{1,9},... | collective-permute-start | bytes 1572872 | tf_op jit(solution)/shard_map/ppermute | solution.py:13
  41.2 8.3 %collective-permute-start.5 = (bf16[1024,256]{1,0:T(8,128)(2,1)}, bf16[1024,256]{1,0:T(8,128)(2,1)}, u32[]{:S(2)}, u32[]{:S(2)}) collective-permute-start(bf16[1024,256]{1,0:T(8,128)(2,1)} %collective-permute-done.4), channel_id=1, source_target_pairs={{0,56},{8,0},{16,8},{24,16},{32,24},{40,32},{48,40},{56,48},{1,57}... | collective-permute-start | bytes 1572872 | tf_op jit(solution)/shard_map/ppermute | solution.py:15
  49.1 8.9 %collective-permute-start.3 = (bf16[1024,256]{1,0:T(8,128)(2,1)}, bf16[1024,256]{1,0:T(8,128)(2,1)}, u32[]{:S(2)}, u32[]{:S(2)}) collective-permute-start(bf16[1024,256]{1,0:T(8,128)(2,1)} %collective-permute-done.2), channel_id=1, source_target_pairs={{0,8},{8,16},{16,24},{24,32},{32,40},{40,48},{48,56},{56,0},{1,9},... | collective-permute-start | bytes 1572872 | tf_op jit(solution)/shard_map/ppermute | solution.py:13
  49.1 16.6 %copy-start.2 = (bf16[1024,256]{1,0:T(8,128)(2,1)S(1)}, bf16[1024,256]{1,0:T(8,128)(2,1)}, u32[]{:S(2)}) copy-start(bf16[1024,256]{1,0:T(8,128)(2,1)} %copy-done.1) | copy-start | bytes 1572868
  49.5 14.1 %collective-permute-start.6 = (bf16[1024,256]{1,0:T(8,128)(2,1)}, bf16[1024,256]{1,0:T(8,128)(2,1)S(1)}, u32[]{:S(2)}, u32[]{:S(2)}) collective-permute-start(bf16[1024,256]{1,0:T(8,128)(2,1)} %collective-permute-done.5), channel_id=1, source_target_pairs={{0,56},{8,0},{16,8},{24,16},{32,24},{40,32},{48,40},{56,48},{1,57}... | collective-permute-start | bytes 1572872 | tf_op jit(solution)/shard_map/ppermute | solution.py:15
